TPU v7x, 32 devices: a whole 2x2x4 slice. The times are simulated.
32 devices in a mesh: owner: 4 (over y, x), rows: 8 (over z, core).
Axes of the slice: x: 2, y: 2, z: 4, core: 2. Of those that a mesh axis runs over, the one named last changes fastest.
Arguments:
- w_gate: float32 [64, 2048, 1024], P('owner', 'rows'), may hold values from -0.1875 to 0.1875
- avg_gate: bfloat16 [64, 2048, 1024], P('owner', 'rows'), may hold values from -0.0625 to 0.0625
- w_up: float32 [64, 2048, 1024], P('owner', 'rows'), may hold values from -0.1875 to 0.1875
- avg_up: bfloat16 [64, 2048, 1024], P('owner', 'rows'), may hold values from -0.0625 to 0.0625
- w_down: float32 [64, 1024, 2048], P('owner', None, 'rows'), may hold values from -0.25 to 0.25
- avg_down: bfloat16 [64, 1024, 2048], P('owner', None, 'rows'), may hold values from -0.09375 to 0.09375
- router_weight: float32 [2048, 64], P('rows', 'owner'), may hold values from -0.125 to 0.125
- router_gain: float32 [2048], P('rows'), may hold values from 0.25 to 1.75
Outputs:
- serve_gate: bfloat16 [64, 2048, 1024], P('owner', None, 'rows')
- serve_up: bfloat16 [64, 2048, 1024], P('owner', None, 'rows')
- serve_down: bfloat16 [64, 1024, 2048], P('owner', 'rows')
- scale_gate: float32 [64, 1024], P('owner', 'rows')
- scale_up: float32 [64, 1024], P('owner', 'rows')
- scale_down: float32 [64, 1024], P('owner', 'rows')
- serve_router: bfloat16 [2048, 64], replicated
All inputs are finite; a program needn't handle non-finite values.
Results may differ from a plain program's by a relative error of at most 0.0015.
Values may be sent and summed in bfloat16 or wider, within the bound.
A program may use at most 192 MiB of HBM per device.

v0:
```python
import jax
import jax.numpy as jnp
from jax import lax
from jax.sharding import PartitionSpec as P


def shards(w_gate, avg_gate, w_up, avg_up, w_down, avg_down, router_weight, router_gain):
    fresh_gate = w_gate + avg_gate.astype(jnp.float32)
    fresh_up = w_up + avg_up.astype(jnp.float32)
    fresh_down = w_down + avg_down.astype(jnp.float32)
    total_gate, total_up, total_down = lax.psum(
        (
            jnp.sum(fresh_gate * fresh_gate, axis=1),
            jnp.sum(fresh_up * fresh_up, axis=1),
            jnp.sum(fresh_down * fresh_down, axis=2),
        ),
        "rows",
    )
    scale_gate = jnp.sqrt(total_gate)
    scale_up = jnp.sqrt(total_up)
    scale_down = jnp.sqrt(total_down)
    narrow_gate, narrow_up, narrow_down = (
        (fresh_gate / jnp.expand_dims(scale_gate, 1)).astype(jnp.bfloat16),
        (fresh_up / jnp.expand_dims(scale_up, 1)).astype(jnp.bfloat16),
        (fresh_down / jnp.expand_dims(scale_down, 2)).astype(jnp.bfloat16),
    )
    serve_gate, serve_up = (
        lax.all_to_all(narrow_gate, "rows", split_axis=2, concat_axis=1, tiled=True),
        lax.all_to_all(narrow_up, "rows", split_axis=2, concat_axis=1, tiled=True),
    )
    serve_down = lax.all_to_all(narrow_down, "rows", split_axis=1, concat_axis=2, tiled=True)
    scale_gate = lax.dynamic_slice_in_dim(
        scale_gate, lax.axis_index("rows") * serve_gate.shape[2], serve_gate.shape[2], axis=1
    )
    scale_up = lax.dynamic_slice_in_dim(
        scale_up, lax.axis_index("rows") * serve_up.shape[2], serve_up.shape[2], axis=1
    )
    scale_down = lax.dynamic_slice_in_dim(
        scale_down, lax.axis_index("rows") * serve_down.shape[1], serve_down.shape[1], axis=1
    )
    part_router = (router_weight * router_gain[:, None]).astype(jnp.bfloat16)
    row_router = lax.all_gather(part_router, "rows", axis=0, tiled=True)
    serve_router = lax.all_gather(row_router, "owner", axis=1, tiled=True)
    return (serve_gate, serve_up, serve_down, scale_gate, scale_up, scale_down, serve_router)


def solution(mesh):
    return jax.shard_map(
        shards,
        mesh=mesh,
        in_specs=(
            P("owner", "rows", None),
            P("owner", "rows", None),
            P("owner", "rows", None),
            P("owner", "rows", None),
            P("owner", None, "rows"),
            P("owner", None, "rows"),
            P("rows", "owner"),
            P("rows"),
        ),
        out_specs=(
            P("owner", None, "rows"),
            P("owner", None, "rows"),
            P("owner", "rows", None),
            P("owner", "rows"),
            P("owner", "rows"),
            P("owner", "rows"),
            P(),
        ),
        check_vma=False,
    )
```

profile of v0, /device:TPU:0, one launch (start us, length us, event | category | flops | bytes accessed | tf_op | source)
XLA Modules:
  0.0 824.8 jit_solution(4685212397091970850)
XLA Ops:
  7.2 17.6 %copy.31 = f32[16,256,1024]{1,0,2:T(8,128)} copy(f32[16,256,1024]{2,1,0:T(8,128)} %param.8) | data formatting | bytes 33554432 | tf_op args[0]
  24.8 17.6 %copy.34 = f32[16,256,1024]{1,0,2:T(8,128)} copy(f32[16,256,1024]{2,1,0:T(8,128)} %param.10) | data formatting | bytes 33554432 | tf_op args[2]
  42.4 12.5 %copy.30 = bf16[16,256,1024]{1,0,2:T(8,128)(2,1)} copy(bf16[16,256,1024]{2,1,0:T(8,128)(2,1)} %param.9) | data formatting | bytes 16777216 | tf_op args[1]
  54.9 12.5 %copy.33 = bf16[16,256,1024]{1,0,2:T(8,128)(2,1)} copy(bf16[16,256,1024]{2,1,0:T(8,128)(2,1)} %param.11) | data formatting | bytes 16777216 | tf_op args[3]
  67.4 25.2 %multiply_reduce_fusion = f32[16,1024]{0,1:T(8,128)} fusion(f32[16,1024,256]{2,1,0:T(8,128)} %param.12, bf16[16,1024,256]{2,1,0:T(8,128)(2,1)} %param.13), kind=kLoop, calls=%fused_computation.2 | loop fusion | flops 16760832 | bytes 25231360 | tf_op jit(solution)/shard_map/reduce_sum | solution.py:15
  92.6 13.2 %multiply_reduce_fusion.1 = (f32[16,1024]{0,1:T(8,128)}, f32[16,1024]{0,1:T(8,128)}) fusion(f32[16,256,1024]{1,0,2:T(8,128)} %copy.34, bf16[16,256,1024]{1,0,2:T(8,128)(2,1)S(1)} %copy-done.1, f32[16,256,1024]{1,0,2:T(8,128)} %copy.31, bf16[16,256,1024]{1,0,2:T(8,128)(2,1)S(1)} %copy-done), kind=kLoop, calls=%fused_computation.4 | loop fusion | flops 33521664 | bytes 50462720 | tf_op jit(solution)/shard_map/reduce_sum | solution.py:14
  105.8 65.1 %all-reduce.3.cloned.1.call-done = (f32[16,1024]{0,1:T(8,128)}, f32[16,1024]{0,1:T(8,128)}, f32[16,1024]{0,1:T(8,128)}) async-done(((f32[16,1024]{0,1:T(8,128)}, f32[16,1024]{0,1:T(8,128)}, f32[16,1024]{0,1:T(8,128)}), (f32[16,1024]{0,1:T(8,128)}, f32[16,1024]{0,1:T(8,128)}, f32[16,1024]{0,1:T(8,128)})) %all-reduce.3.cloned.1.call-update) | async-done | bytes 196624 | tf_op jit(solution)/shard_map/psum | solution.py:11
  170.9 1.2 sqrt.10
  172.1 12.0 %divide_convert_fusion.1 = bf16[16,256,1024]{1,0,2:T(8,128)(2,1)} fusion(f32[16,256,1024]{1,0,2:T(8,128)} %copy.34, bf16[16,256,1024]{1,0,2:T(8,128)(2,1)} %copy.33, f32[16,1024]{0,1:T(8,128)S(1)} %sqrt.10), kind=kLoop, calls=%fused_computation.3 | loop fusion | flops 16777216 | bytes 33619968 | tf_op jit(solution)/shard_map/convert_element_type | solution.py:24
  184.1 5.1 all-to-all-start.1
  189.3 12.0 %divide_convert_fusion.2 = bf16[16,256,1024]{1,0,2:T(8,128)(2,1)} fusion(f32[16,256,1024]{1,0,2:T(8,128)} %copy.31, bf16[16,256,1024]{1,0,2:T(8,128)(2,1)} %copy.30, f32[16,1024]{0,1:T(8,128)S(1)} %sqrt.9), kind=kLoop, calls=%fused_computation.6 | loop fusion | flops 16777216 | bytes 33619968 | tf_op jit(solution)/shard_map/convert_element_type | solution.py:23
  201.3 171.7 %all-to-all-done.1 = bf16[16,256,1024]{1,0,2:T(8,128)(2,1)} async-done(((bf16[16,256,1024]{1,0,2:T(8,128)(2,1)}), bf16[16,256,1024]{1,0,2:T(8,128)(2,1)}, u32[]{:S(2)}, u32[]{:S(2)}) %all-to-all-start.1) | async-done | bytes 8388640 | tf_op jit(solution)/shard_map/all_to_all | solution.py:29
  373.0 5.1 all-to-all-start
  378.3 23.8 %divide_convert_fusion = bf16[16,1024,256]{2,0,1:T(8,128)(2,1)} fusion(f32[16,1024,256]{2,1,0:T(8,128)} %param.12, f32[16,1024]{0,1:T(8,128)S(1)} %sqrt.11, bf16[16,1024,256]{2,1,0:T(8,128)(2,1)} %param.13), kind=kLoop, calls=%fused_computation.1 | loop fusion | flops 16777216 | bytes 33619968 | tf_op jit(solution)/shard_map/convert_element_type | solution.py:25
  402.1 159.8 %all-to-all-done = bf16[16,256,1024]{1,0,2:T(8,128)(2,1)} async-done(((bf16[16,256,1024]{1,0,2:T(8,128)(2,1)}), bf16[16,256,1024]{1,0,2:T(8,128)(2,1)}, u32[]{:S(2)}, u32[]{:S(2)}) %all-to-all-start) | async-done | bytes 8388640 | tf_op jit(solution)/shard_map/all_to_all | solution.py:28
  561.8 5.0 all-to-all-start.2
  566.9 189.9 %all_gather.6 = bf16[2048,16]{0,1:T(8,128)(2,1)S(1)} all-gather(bf16[256,16]{0,1:T(8,128)(2,1)S(1)} %multiply_convert_fusion), channel_id=1, replica_groups=mesh['owner'=4,'rows'=8] {'rows'}, dimensions={0}, use_global_device_ids=true | all-gather | bytes 73728 | tf_op jit(solution)/shard_map/all_gather | solution.py:42
  756.8 9.1 %all_gather.7 = bf16[2048,64]{0,1:T(8,128)(2,1)S(1)} all-gather(bf16[2048,16]{0,1:T(8,128)(2,1)S(1)} %all_gather.6), channel_id=1, replica_groups=mesh['owner'=4,'rows'=8] {'owner'}, dimensions={1}, use_global_device_ids=true | all-gather | bytes 327680 | tf_op jit(solution)/shard_map/all_gather | solution.py:43
  765.9 0.7 copy.39
  767.9 12.3 %copy.35 = bf16[16,8,256,128]{3,2,1,0:T(8,128)(2,1)} copy(bf16[16,8,256,128]{2,0,3,1:T(8,128)(2,1)} %bitcast.4) | data formatting | bytes 16777216 | tf_op jit(solution)/shard_map/all_to_all | solution.py:29
  780.2 12.3 %copy.32 = bf16[16,8,256,128]{3,2,1,0:T(8,128)(2,1)} copy(bf16[16,8,256,128]{2,0,3,1:T(8,128)(2,1)} %bitcast.1) | data formatting | bytes 16777216 | tf_op jit(solution)/shard_map/all_to_all | solution.py:28
  792.5 11.4 %copy.38 = bf16[16,128,8,256]{3,2,1,0:T(8,128)(2,1)} copy(bf16[16,128,8,256]{3,0,1,2:T(8,128)(2,1)} %bitcast.7) | data formatting | bytes 16777216 | tf_op jit(solution)/shard_map/all_to_all | solution.py:31
  803.9 13.4 %all_to_all.50 = bf16[16,128,2048]{2,1,0:T(8,128)(2,1)} reshape(bf16[16,128,8,256]{3,2,1,0:T(8,128)(2,1)} %copy.38) | data formatting | bytes 16777216 | tf_op jit(solution)/shard_map/all_to_all | solution.py:31
  817.3 0.7 copy.53
  (23 shorter events, 1.7 us)
Async XLA Ops:
  7.2 163.7 %all-reduce.3.cloned.1.call-start = ((), (), s32[]{:S(2)}) async-start(), calls=%async_computation.3 | async-start | bytes 3145728 | tf_op jit(solution)/shard_map/psum | solution.py:11
  67.4 25.2 %copy-start = (bf16[16,256,1024]{1,0,2:T(8,128)(2,1)S(1)}, bf16[16,256,1024]{1,0,2:T(8,128)(2,1)}, u32[]{:S(2)}) copy-start(bf16[16,256,1024]{1,0,2:T(8,128)(2,1)} %copy.30) | copy-start | bytes 25165828
  67.4 25.2 %copy-start.1 = (bf16[16,256,1024]{1,0,2:T(8,128)(2,1)S(1)}, bf16[16,256,1024]{1,0,2:T(8,128)(2,1)}, u32[]{:S(2)}) copy-start(bf16[16,256,1024]{1,0,2:T(8,128)(2,1)} %copy.33) | copy-start | bytes 25165828
  184.1 5.1 copy-start.3
  184.1 189.0 %all-to-all-start.1 = ((bf16[16,256,1024]{1,0,2:T(8,128)(2,1)}), bf16[16,256,1024]{1,0,2:T(8,128)(2,1)}, u32[]{:S(2)}, u32[]{:S(2)}) async-start(bf16[16,256,1024]{1,0,2:T(8,128)(2,1)} %divide_convert_fusion.1), calls=%async_computation.1 | async-start | bytes 16777216 | tf_op jit(solution)/shard_map/all_to_all | solution.py:29
  201.3 176.9 %copy-start.2 = (f32[16,1024]{0,1:T(8,128)S(1)}, f32[16,1024]{0,1:T(8,128)}, u32[]{:S(2)}) copy-start(f32[16,1024]{0,1:T(8,128)} %get-tuple-element.16) | copy-start | bytes 196612
  373.0 188.8 %all-to-all-start = ((bf16[16,256,1024]{1,0,2:T(8,128)(2,1)}), bf16[16,256,1024]{1,0,2:T(8,128)(2,1)}, u32[]{:S(2)}, u32[]{:S(2)}) async-start(bf16[16,256,1024]{1,0,2:T(8,128)(2,1)} %divide_convert_fusion.2), calls=%async_computation | async-start | bytes 16777216 | tf_op jit(solution)/shard_map/all_to_all | solution.py:28
  402.1 164.8 %copy-start.4 = (f32[256,16]{0,1:T(8,128)S(1)}, f32[256,16]{0,1:T(8,128)}, u32[]{:S(2)}) copy-start(f32[256,16]{0,1:T(8,128)} %param.14) | copy-start | bytes 49156
  402.1 164.8 %copy-start.5 = (f32[256]{0:T(256)S(1)}, f32[256]{0:T(256)}, u32[]{:S(2)}) copy-start(f32[256]{0:T(256)} %param.15) | copy-start | bytes 3076
  561.8 230.7 %all-to-all-start.2 = ((bf16[16,1024,256]{2,0,1:T(8,128)(2,1)}), bf16[16,1024,256]{2,0,1:T(8,128)(2,1)}, u32[]{:S(2)}, u32[]{:S(2)}) async-start(bf16[16,1024,256]{2,0,1:T(8,128)(2,1)} %divide_convert_fusion), calls=%async_computation.2 | async-start | bytes 16777216 | tf_op jit(solution)/shard_map/all_to_all | solution.py:31
Sparse Core Ops, SparseCore 0:
  105.9 64.9 all-reduce.2
where the time goes:
time: 827 us; the launch traced here: 825 us
  waiting for transfers between devices  397 us (48%)
  blocking collectives  199 us (24%)
  local copies, waits for them, and re-layouts  114 us (14%)
  other arithmetic  86.1 us (10%)
  starting transfers between devices  15.3 us (2%)
  between operations  14.1 us (2%)
    all_gather x1, blocking collectives, shards(): row_router = lax.all_gather(part_router, 'rows', axis=0, tiled=True)  190 us
    all_to_all x1, waiting for transfers between devices, shards(): lax.all_to_all(narrow_up, 'rows', split_axis=2, concat_axis=1, tiled=True)  172 us
    all_to_all x1, waiting for transfers between devices, shards(): lax.all_to_all(narrow_gate, 'rows', split_axis=2, concat_axis=1, tiled=True)  160 us
    psum x1, waiting for transfers between devices, shards(): lax.psum((jnp.sum(fresh_gate * fresh_gate, axis=1), jnp.sum(fresh_up * fr...  65.1 us
    unnamed x20, local copies, waits for them, and re-layouts  62.9 us
    reduce_sum x1, other arithmetic, shards(): jnp.sum(fresh_down * fresh_down, axis=2)  25.2 us
    all_to_all x2, local copies, waits for them, and re-layouts, shards(): lax.all_to_all(narrow_down, 'rows', split_axis=1, concat_axis=2, tiled=True)  24.8 us
    convert_element_type x1, other arithmetic, shards(): (fresh_down / jnp.expand_dims(scale_down, 2)).astype(jnp.bfloat16)  23.8 us
  transfers between devices with their start and end apart: 4, of which 3 were waited for; matrix products, arithmetic and copies ran while one was open for 8% of the time, Pallas kernels for 0%

commit v1 on v0

--- a/solution.py
+++ b/solution.py
@@ -2,6 +2,13 @@
 import jax.numpy as jnp
 from jax import lax
 from jax.sharding import PartitionSpec as P
+
+
+def write_marks_on(x0, axis_id):
+    return jnp.concatenate(
+        lax.all_to_all(jnp.stack(jnp.split(x0, lax.psum(1, axis_id), axis=2)), axis_id, 0, 0),
+        axis=1,
+    )
 
 
 def shards(w_gate, avg_gate, w_up, avg_up, w_down, avg_down, router_weight, router_gain):
@@ -25,7 +32,7 @@
         (fresh_down / jnp.expand_dims(scale_down, 2)).astype(jnp.bfloat16),
     )
     serve_gate, serve_up = (
-        lax.all_to_all(narrow_gate, "rows", split_axis=2, concat_axis=1, tiled=True),
+        write_marks_on(narrow_gate, "rows"),
         lax.all_to_all(narrow_up, "rows", split_axis=2, concat_axis=1, tiled=True),
     )
     serve_down = lax.all_to_all(narrow_down, "rows", split_axis=1, concat_axis=2, tiled=True)

time: 827 us -> 791 us (0.956)
  local copies, waits for them, and re-layouts: 114 us -> 89 us
  waiting for transfers between devices: 397 us -> 387 us
    all_to_all x1, waiting for transfers between devices: 0.01 us -> 164 us  [shards(): lax.all_to_all(narrow_down, 'rows', split_axis=1, concat_axis=2, tiled=True)]
    all_to_all x1, waiting for transfers between devices: 160 us -> 0.01 us  [write_marks_on(): lax.all_to_all(jnp.stack(jnp.split(x0, lax.psum(1, axis_id), axis=2)), ax...]
    unnamed x20 -> x34, local copies, waits for them, and re-layouts: 62.9 us -> 40.9 us
    all_to_all x1 -> x0, local copies, waits for them, and re-layouts: 12.3 us -> none  [shards(): lax.all_to_all(narrow_gate, 'rows', split_axis=2, concat_axis=1, tiled=True)]
    all_to_all x1, waiting for transfers between devices: 172 us -> 160 us  [shards(): lax.all_to_all(narrow_up, 'rows', split_axis=2, concat_axis=1, tiled=True)]
    reduce_sum x0 -> x1, other arithmetic: none -> 10.6 us  [shards(): jnp.sum(fresh_gate * fresh_gate, axis=1)]
    reduce_sum x1, other arithmetic: 13.2 us -> 4.34 us  [shards(): jnp.sum(fresh_up * fresh_up, axis=1)]
  transfers between devices with their start and end apart: 4 -> 4, of which waited for: 3 -> 3; matrix products, arithmetic and copies ran while one was open for 8% -> 9% of each run, Pallas kernels for 0% -> 0%
where the time goes in v1:
time: 791 us; the launch traced here: 789 us
  waiting for transfers between devices  387 us (49%)
  blocking collectives  199 us (25%)
  local copies, waits for them, and re-layouts  89 us (11%)
  other arithmetic  84.7 us (11%)
  starting transfers between devices  15.3 us (2%)
  between operations  14.2 us (2%)
    all_gather x1, blocking collectives, shards(): row_router = lax.all_gather(part_router, 'rows', axis=0, tiled=True)  190 us
    all_to_all x1, waiting for transfers between devices, shards(): lax.all_to_all(narrow_down, 'rows', split_axis=1, concat_axis=2, tiled=True)  164 us
    all_to_all x1, waiting for transfers between devices, shards(): lax.all_to_all(narrow_up, 'rows', split_axis=2, concat_axis=1, tiled=True)  160 us
    psum x1, waiting for transfers between devices, shards(): lax.psum((jnp.sum(fresh_gate * fresh_gate, axis=1), jnp.sum(fresh_up * fr...  62.6 us
    unnamed x34, local copies, waits for them, and re-layouts  40.9 us
    all_to_all x2, local copies, waits for them, and re-layouts, shards(): lax.all_to_all(narrow_down, 'rows', split_axis=1, concat_axis=2, tiled=True)  24.8 us
    reduce_sum x1, other arithmetic, shards(): jnp.sum(fresh_down * fresh_down, axis=2)  24.6 us
    convert_element_type x1, other arithmetic, shards(): (fresh_down / jnp.expand_dims(scale_down, 2)).astype(jnp.bfloat16)  23.8 us
  transfers between devices with their start and end apart: 4, of which 3 were waited for; matrix products, arithmetic and copies ran while one was open for 9% of the time, Pallas kernels for 0%

profile of v1, /device:TPU:0, one launch (start us, length us, event | category | flops | bytes accessed | tf_op | source)
XLA Modules:
  0.0 789.0 jit_solution(4520369092743525560)
XLA Ops:
  7.2 12.5 %copy.28 = bf16[16,256,1024]{1,0,2:T(8,128)(2,1)} copy(bf16[16,256,1024]{2,1,0:T(8,128)(2,1)} %param.11) | data formatting | bytes 16777216 | tf_op args[3]
  19.7 17.6 %copy.29 = f32[16,256,1024]{1,0,2:T(8,128)} copy(f32[16,256,1024]{2,1,0:T(8,128)} %param.10) | data formatting | bytes 33554432 | tf_op args[2]
  37.3 10.6 %multiply_reduce_fusion.2 = f32[16,1024]{1,0:T(8,128)} fusion(f32[16,256,1024]{2,1,0:T(8,128)} %param.8, bf16[16,256,1024]{2,1,0:T(8,128)(2,1)} %param.9), kind=kLoop, calls=%fused_computation.7 | loop fusion | flops 16760832 | bytes 25231360 | tf_op jit(solution)/shard_map/reduce_sum | solution.py:20
  47.9 24.6 %multiply_reduce_fusion = f32[16,1024]{0,1:T(8,128)} fusion(f32[16,1024,256]{2,1,0:T(8,128)} %param.12, bf16[16,1024,256]{2,1,0:T(8,128)(2,1)S(1)} %copy-done), kind=kLoop, calls=%fused_computation.2 | loop fusion | flops 16760832 | bytes 25231360 | tf_op jit(solution)/shard_map/reduce_sum | solution.py:22
  72.5 4.3 multiply_reduce_fusion.1
  76.9 62.6 %all-reduce.3.cloned.1.call-done = (f32[16,1024]{1,0:T(8,128)}, f32[16,1024]{0,1:T(8,128)}, f32[16,1024]{0,1:T(8,128)}) async-done(((f32[16,1024]{1,0:T(8,128)}, f32[16,1024]{0,1:T(8,128)}, f32[16,1024]{0,1:T(8,128)}), (f32[16,1024]{1,0:T(8,128)}, f32[16,1024]{0,1:T(8,128)}, f32[16,1024]{0,1:T(8,128)})) %all-reduce.3.cloned.1.call-update) | async-done | bytes 196624 | tf_op jit(solution)/shard_map/psum | solution.py:18
  140.7 12.0 %divide_convert_fusion.1 = bf16[16,256,1024]{1,0,2:T(8,128)(2,1)} fusion(f32[16,256,1024]{1,0,2:T(8,128)} %copy.29, bf16[16,256,1024]{1,0,2:T(8,128)(2,1)} %copy.28, f32[16,1024]{0,1:T(8,128)S(1)} %sqrt.10), kind=kLoop, calls=%fused_computation.3 | loop fusion | flops 16777216 | bytes 33619968 | tf_op jit(solution)/shard_map/convert_element_type | solution.py:31
  152.7 5.3 all-to-all-start.1
  158.2 23.8 %divide_convert_fusion = bf16[16,1024,256]{2,0,1:T(8,128)(2,1)} fusion(f32[16,1024,256]{2,1,0:T(8,128)} %param.12, f32[16,1024]{0,1:T(8,128)S(1)} %sqrt.11, bf16[16,1024,256]{2,1,0:T(8,128)(2,1)} %param.13), kind=kLoop, calls=%fused_computation.1 | loop fusion | flops 16777216 | bytes 33619968 | tf_op jit(solution)/shard_map/convert_element_type | solution.py:32
  182.0 159.7 %all-to-all-done.1 = bf16[16,256,1024]{1,0,2:T(8,128)(2,1)} async-done(((bf16[16,256,1024]{1,0,2:T(8,128)(2,1)}), bf16[16,256,1024]{1,0,2:T(8,128)(2,1)}, u32[]{:S(2)}, u32[]{:S(2)}) %all-to-all-start.1) | async-done | bytes 8388640 | tf_op jit(solution)/shard_map/all_to_all | solution.py:36
  341.7 5.0 all-to-all-start.2
  346.7 9.4 %divide_convert_fusion.2 = bf16[16,256,1024]{2,1,0:T(8,128)(2,1)S(1)} fusion(f32[16,256,1024]{2,1,0:T(8,128)} %param.8, bf16[16,256,1024]{2,1,0:T(8,128)(2,1)} %param.9, f32[16,1024]{1,0:T(8,128)S(1)} %sqrt.9), kind=kLoop, calls=%fused_computation.6 | loop fusion | flops 16777216 | bytes 33619968 | tf_op jit(solution)/shard_map/convert_element_type | solution.py:30
  356.1 1.2 fusion.7
  358.6 1.2 fusion.5
  359.9 1.2 fusion.4
  361.1 1.2 fusion.3
  366.1 164.4 %all-to-all-done.2 = bf16[16,1024,256]{2,0,1:T(8,128)(2,1)} async-done(((bf16[16,1024,256]{2,0,1:T(8,128)(2,1)}), bf16[16,1024,256]{2,0,1:T(8,128)(2,1)}, u32[]{:S(2)}, u32[]{:S(2)}) %all-to-all-start.2) | async-done | bytes 8388640 | tf_op jit(solution)/shard_map/all_to_all | solution.py:38
  530.5 5.0 all-to-all-start
  535.5 189.9 %all_gather.6 = bf16[2048,16]{0,1:T(8,128)(2,1)S(1)} all-gather(bf16[256,16]{0,1:T(8,128)(2,1)S(1)} %multiply_convert_fusion), channel_id=1, replica_groups=mesh['owner'=4,'rows'=8] {'rows'}, dimensions={0}, use_global_device_ids=true | all-gather | bytes 73728 | tf_op jit(solution)/shard_map/all_gather | solution.py:49
  725.4 9.1 %all_gather.7 = bf16[2048,64]{0,1:T(8,128)(2,1)S(1)} all-gather(bf16[2048,16]{0,1:T(8,128)(2,1)S(1)} %all_gather.6), channel_id=1, replica_groups=mesh['owner'=4,'rows'=8] {'owner'}, dimensions={1}, use_global_device_ids=true | all-gather | bytes 327680 | tf_op jit(solution)/shard_map/all_gather | solution.py:50
  736.5 12.3 %copy.30 = bf16[16,8,256,128]{3,2,1,0:T(8,128)(2,1)} copy(bf16[16,8,256,128]{2,0,3,1:T(8,128)(2,1)} %bitcast.11) | data formatting | bytes 16777216 | tf_op jit(solution)/shard_map/all_to_all | solution.py:36
  748.8 11.4 %copy.33 = bf16[16,128,8,256]{3,2,1,0:T(8,128)(2,1)} copy(bf16[16,128,8,256]{3,0,1,2:T(8,128)(2,1)} %bitcast.14) | data formatting | bytes 16777216 | tf_op jit(solution)/shard_map/all_to_all | solution.py:38
  760.2 13.4 %all_to_all.37 = bf16[16,128,2048]{2,1,0:T(8,128)(2,1)} reshape(bf16[16,128,8,256]{3,2,1,0:T(8,128)(2,1)} %copy.33) | data formatting | bytes 16777216 | tf_op jit(solution)/shard_map/all_to_all | solution.py:38
  773.6 7.9 copy.27
  (40 shorter events, 9.0 us)
Async XLA Ops:
  7.2 132.4 %all-reduce.3.cloned.1.call-start = ((), (), s32[]{:S(2)}) async-start(), calls=%async_computation.3 | async-start | bytes 2228224 | tf_op jit(solution)/shard_map/psum | solution.py:18
  37.3 10.7 %copy-start = (bf16[16,1024,256]{2,1,0:T(8,128)(2,1)S(1)}, bf16[16,1024,256]{2,1,0:T(8,128)(2,1)}, u32[]{:S(2)}) copy-start(bf16[16,1024,256]{2,1,0:T(8,128)(2,1)} %param.13) | copy-start | bytes 25165828
  37.3 35.2 %slice-start = ((s8[16777216]{0:T(1024)(128)(4,1)}), s8[4194304]{0:T(1024)(128)(4,1)S(1)}, s32[]{:S(2)}) async-start(s8[16777216]{0:T(1024)(128)(4,1)} %bitcast.43), calls=%async_computation.4 | async-start | bytes 8388608
  37.3 35.2 %slice-start.1 = ((s8[16777216]{0:T(1024)(128)(4,1)}), s8[4194304]{0:T(1024)(128)(4,1)S(1)}, s32[]{:S(2)}) async-start(s8[16777216]{0:T(1024)(128)(4,1)} %bitcast.43), calls=%async_computation.5 | async-start | bytes 8388608
  37.3 35.2 %slice-start.4 = ((s8[8388608]{0:T(1024)(128)(4,1)}), s8[4194304]{0:T(1024)(128)(4,1)S(1)}, s32[]{:S(2)}) async-start(s8[8388608]{0:T(1024)(128)(4,1)} %bitcast.45), calls=%async_computation.8 | async-start | bytes 8388608
  47.9 24.6 %slice-start.2 = ((s8[16777216]{0:T(1024)(128)(4,1)}), s8[4194304]{0:T(1024)(128)(4,1)S(1)}, s32[]{:S(2)}) async-start(s8[16777216]{0:T(1024)(128)(4,1)} %bitcast.43), calls=%async_computation.6 | async-start | bytes 8388608
  47.9 24.6 %slice-start.3 = ((s8[16777216]{0:T(1024)(128)(4,1)}), s8[4194304]{0:T(1024)(128)(4,1)S(1)}, s32[]{:S(2)}) async-start(s8[16777216]{0:T(1024)(128)(4,1)} %bitcast.43), calls=%async_computation.7 | async-start | bytes 8388608
  47.9 24.6 %slice-start.5 = ((s8[8388608]{0:T(1024)(128)(4,1)}), s8[4194304]{0:T(1024)(128)(4,1)S(1)}, s32[]{:S(2)}) async-start(s8[8388608]{0:T(1024)(128)(4,1)} %bitcast.45), calls=%async_computation.9 | async-start | bytes 8388608
  152.7 5.3 copy-start.1
  152.7 189.0 %all-to-all-start.1 = ((bf16[16,256,1024]{1,0,2:T(8,128)(2,1)}), bf16[16,256,1024]{1,0,2:T(8,128)(2,1)}, u32[]{:S(2)}, u32[]{:S(2)}) async-start(bf16[16,256,1024]{1,0,2:T(8,128)(2,1)} %divide_convert_fusion.1), calls=%async_computation.1 | async-start | bytes 16777216 | tf_op jit(solution)/shard_map/all_to_all | solution.py:36
  182.0 164.7 %copy-start.2 = (f32[16,1024]{1,0:T(8,128)S(1)}, f32[16,1024]{1,0:T(8,128)}, u32[]{:S(2)}) copy-start(f32[16,1024]{1,0:T(8,128)} %get-tuple-element.14) | copy-start | bytes 196612
  341.7 188.8 %all-to-all-start.2 = ((bf16[16,1024,256]{2,0,1:T(8,128)(2,1)}), bf16[16,1024,256]{2,0,1:T(8,128)(2,1)}, u32[]{:S(2)}, u32[]{:S(2)}) async-start(bf16[16,1024,256]{2,0,1:T(8,128)(2,1)} %divide_convert_fusion), calls=%async_computation.2 | async-start | bytes 16777216 | tf_op jit(solution)/shard_map/all_to_all | solution.py:38
  366.1 169.4 %copy-start.3 = (f32[256,16]{0,1:T(8,128)S(1)}, f32[256,16]{0,1:T(8,128)}, u32[]{:S(2)}) copy-start(f32[256,16]{0,1:T(8,128)} %param.14) | copy-start | bytes 49156
  366.1 169.4 %copy-start.4 = (f32[256]{0:T(256)S(1)}, f32[256]{0:T(256)}, u32[]{:S(2)}) copy-start(f32[256]{0:T(256)} %param.15) | copy-start | bytes 3076
  530.5 243.1 %all-to-all-start = ((bf16[8,16,256,128]{3,2,1,0:T(8,128)(2,1)}), bf16[8,16,256,128]{3,2,1,0:T(8,128)(2,1)}, u32[]{:S(2)}, u32[]{:S(2)}) async-start(bf16[8,16,256,128]{3,2,1,0:T(8,128)(2,1)} %fusion), calls=%async_computation | async-start | bytes 16777216 | tf_op jit(solution)/shard_map/all_to_all | solution.py:9
Sparse Core Ops, SparseCore 0:
  77.0 62.4 all-reduce.2
